TPU v7x, 32 devices: a whole 2x2x4 slice. The times are simulated.
32 devices in a mesh: slab: 2 (over x), py: 4 (over y, core), px: 4 (over z).
Axes of the slice: x: 2, y: 2, z: 4, core: 2. Of those that a mesh axis runs over, the one named last changes fastest.
Arguments:
- state: bfloat16 [2, 3, 16, 1024, 1024], P(None, None, 'slab', ('py', 'px')), may hold values from -12 to 12
- shells: int32 [16, 1024, 1024], P('slab', ('py', 'px')), may hold values from 0 to 511
Outputs:
- restored: float32 [2, 3, 16, 1024, 1024], P(None, None, ('slab', 'py'), None, 'px')
- spectrum: float32 [512], replicated
All inputs are finite; a program needn't handle non-finite values.
Results may differ from a plain program's by a relative error of at most 0.0003.
Values may be sent and summed in bfloat16 or wider, within the bound.
A program may use at most 128 MiB of HBM per device.

v0:
```python
import functools

import jax
import jax.numpy as jnp
from jax import lax
from jax.experimental import pallas as pl
from jax.experimental.pallas import tpu as pltpu
from jax.sharding import PartitionSpec as P

SHELLS = 512
LOW = 32
HIGH = SHELLS // LOW
LANES = 128
SPEC_ROWS = SHELLS // LANES
GROUP_ROWS = 16
MESH = pl.DeviceIdType.MESH


def kernel(
    slab_count,
    py_count,
    px_count,
    state,
    shells,
    out,
    spec,
    modes,
    labels,
    slab_parts,
    group_parts,
    state_sem,
    label_sem,
    own_sem,
    send_sem,
    recv_sem,
    slab_send,
    slab_recv,
    part_send,
    part_recv,
):
    slab = lax.axis_index("slab")
    py = lax.axis_index("py")
    px = lax.axis_index("px")
    group = py_count * px_count
    me = py * px_count + px
    _, _, planes, rows, columns = state.shape
    planes_out = planes // py_count
    columns_out = columns // px_count

    def load_state(z):
        return pltpu.make_async_copy(state.at[:, :, z], modes.at[:, :, z], state_sem.at[z])

    def load_labels(z):
        return pltpu.make_async_copy(shells.at[z], labels.at[z], label_sem.at[z])

    def group_peer(step):
        peer = lax.rem(me + step, group)
        return (peer, peer // px_count, lax.rem(peer, px_count))

    def slab_peer(step):
        return lax.rem(slab + step, slab_count)

    def block(source, dest_py, dest_px):
        return source.at[
            :,
            :,
            pl.ds(dest_py * planes_out, planes_out),
            :,
            pl.ds(pl.multiple_of(dest_px * columns_out, columns_out), columns_out),
        ]

    def landing(source):
        return out.at[:, :, :, pl.ds(pl.multiple_of(source * rows, rows), rows), :]

    def send_block(dest_py, dest_px):
        return pltpu.make_async_remote_copy(
            src_ref=block(state, dest_py, dest_px),
            dst_ref=landing(me),
            send_sem=send_sem.at[dest_py * px_count + dest_px],
            recv_sem=recv_sem.at[me],
            device_id=(slab, dest_py, dest_px),
            device_id_type=MESH,
        )

    def take_block(source, source_py, source_px):
        return pltpu.make_async_remote_copy(
            src_ref=block(state, source_py, source_px),
            dst_ref=landing(source),
            send_sem=send_sem.at[source],
            recv_sem=recv_sem.at[source],
            device_id=(slab, source_py, source_px),
            device_id_type=MESH,
        )

    def send_at(distance):
        for turn in range(py_count):
            dest_py = lax.rem(py + turn, py_count)
            if distance == 0:
                if turn > 0:
                    send_block(dest_py, px).start()
                continue

            @pl.when(px + distance < px_count)
            def _():
                send_block(dest_py, px + distance).start()

            @pl.when(px - distance >= 0)
            def _():
                send_block(dest_py, px - distance).start()

    def slab_copy(dest, slot):
        return pltpu.make_async_remote_copy(
            src_ref=slab_parts.at[slab],
            dst_ref=slab_parts.at[slot],
            send_sem=slab_send.at[dest],
            recv_sem=slab_recv.at[slot],
            device_id=(dest, py, px),
            device_id_type=MESH,
        )

    def part_copy(dest, dest_py, dest_px, slot):
        return pltpu.make_async_remote_copy(
            src_ref=group_parts.at[me],
            dst_ref=group_parts.at[slot],
            send_sem=part_send.at[dest],
            recv_sem=part_recv.at[slot],
            device_id=(slab, dest_py, dest_px),
            device_id_type=MESH,
        )

    for z in range(planes):
        load_state(z).start()
        load_labels(z).start()

    barrier = pltpu.get_barrier_semaphore()
    for step in range(1, group):
        _, peer_py, peer_px = group_peer(step)
        pl.semaphore_signal(
            barrier, inc=1, device_id=(slab, peer_py, peer_px), device_id_type=MESH
        )
    for step in range(1, slab_count):
        pl.semaphore_signal(
            barrier, inc=1, device_id=(slab_peer(step), py, px), device_id_type=MESH
        )
    pl.semaphore_wait(barrier, group - 1 + slab_count - 1)

    for distance in range(px_count - 1, 0, -1):
        send_at(distance)

    low_ids = lax.broadcasted_iota(jnp.int32, (LOW, columns), 0)
    high_ids = lax.broadcasted_iota(jnp.int32, (HIGH, columns), 0)

    def add_rows(z, start, running):
        values = modes[:, :, z, pl.ds(start, GROUP_ROWS), :].astype(jnp.float32)
        energy = 0.5 * jnp.sum(values * values, axis=(0, 1))
        upper = energy.astype(jnp.bfloat16).astype(jnp.float32)
        lower = energy - upper
        numbers = labels[z, pl.ds(start, GROUP_ROWS), :]
        high = numbers >> (LOW.bit_length() - 1)
        low = numbers & (LOW - 1)
        for row in range(GROUP_ROWS):
            one = slice(row, row + 1)
            hot = high_ids == high[one]
            weighted = jnp.concatenate(
                [jnp.where(hot, upper[one], 0.0), jnp.where(hot, lower[one], 0.0)], axis=0
            ).astype(jnp.bfloat16)
            onehot = jnp.where(low_ids == low[one], 1.0, 0.0).astype(jnp.bfloat16)
            running = running + lax.dot_general(
                weighted, onehot, (((1,), (1,)), ((), ())), preferred_element_type=jnp.float32
            )
        return running

    running = jnp.zeros((2 * HIGH, LOW), jnp.float32)
    for z in range(planes):
        load_state(z).wait()
        load_labels(z).wait()

    own = pltpu.make_async_copy(block(state, py, px), landing(me), own_sem)
    own.start()

    groups = rows // GROUP_ROWS
    running = lax.fori_loop(
        0,
        planes * groups,
        lambda i, total: add_rows(
            i // groups, pl.multiple_of(lax.rem(i, groups) * GROUP_ROWS, GROUP_ROWS), total
        ),
        running,
    )
    part = running[:HIGH] + running[HIGH:]
    per_row = LANES // LOW
    for high in range(HIGH):
        lane = (high % per_row) * LOW
        slab_parts[slab, high // per_row : high // per_row + 1, lane : lane + LOW] = part[
            high : high + 1
        ]

    for step in range(1, slab_count):
        slab_copy(slab_peer(step), slab).start()
    for step in range(1, slab_count):
        slab_copy(slab_peer(step), slab_peer(step)).wait_recv()
    total = slab_parts[0]
    for slot in range(1, slab_count):
        total = total + slab_parts[slot]
    group_parts[me] = total
    for step in range(1, group):
        part_copy(*group_peer(step), me).start()

    send_at(0)

    for step in range(1, group):
        peer, peer_py, peer_px = group_peer(step)
        part_copy(peer, peer_py, peer_px, peer).wait_recv()
    total = group_parts[0]
    for slot in range(1, group):
        total = total + group_parts[slot]
    spec[...] = total

    own.wait()
    for step in range(1, slab_count):
        slab_copy(slab_peer(step), slab).wait_send()
    for step in range(1, group):
        peer, peer_py, peer_px = group_peer(step)
        part_copy(peer, peer_py, peer_px, me).wait_send()
        send_block(peer_py, peer_px).wait_send()
        take_block(peer, peer_py, peer_px).wait_recv()


def local(state, shells):
    slab_count = lax.axis_size("slab")
    py_count = lax.axis_size("py")
    px_count = lax.axis_size("px")
    group = py_count * px_count
    _, _, planes, rows, columns = state.shape
    moved, totals = pl.pallas_call(
        functools.partial(kernel, slab_count, py_count, px_count),
        out_shape=(
            pltpu.VMEM(
                (2, 3, planes // py_count, rows * group, columns // px_count), state.dtype
            ),
            jax.ShapeDtypeStruct((SPEC_ROWS, LANES), jnp.float32),
        ),
        in_specs=[pl.BlockSpec(memory_space=pl.ANY)] * 2,
        out_specs=(
            pl.BlockSpec(memory_space=pltpu.VMEM),
            pl.BlockSpec(memory_space=pltpu.VMEM),
        ),
        scratch_shapes=[
            pltpu.VMEM(state.shape, state.dtype),
            pltpu.VMEM(shells.shape, shells.dtype),
            pltpu.VMEM((slab_count, SPEC_ROWS, LANES), jnp.float32),
            pltpu.VMEM((group, SPEC_ROWS, LANES), jnp.float32),
            pltpu.SemaphoreType.DMA((planes,)),
            pltpu.SemaphoreType.DMA((planes,)),
            pltpu.SemaphoreType.DMA,
            pltpu.SemaphoreType.DMA((group,)),
            pltpu.SemaphoreType.DMA((group,)),
            pltpu.SemaphoreType.DMA((slab_count,)),
            pltpu.SemaphoreType.DMA((slab_count,)),
            pltpu.SemaphoreType.DMA((group,)),
            pltpu.SemaphoreType.DMA((group,)),
        ],
        compiler_params=pltpu.CompilerParams(collective_id=0, has_side_effects=True, vmem_limit_bytes=24 << 20),
    )(
        pltpu.with_memory_space_constraint(state, pltpu.HBM),
        pltpu.with_memory_space_constraint(shells, pltpu.HBM),
    )
    modes_all = planes * rows * columns * slab_count * group
    spectrum = totals.reshape(SHELLS) * (SHELLS / modes_all)
    return (moved.astype(jnp.float32), spectrum)


def solution(mesh):
    return jax.shard_map(
        local,
        mesh=mesh,
        in_specs=(P(None, None, "slab", ("py", "px"), None), P("slab", ("py", "px"), None)),
        out_specs=(P(None, None, ("slab", "py"), None, "px"), P()),
        check_vma=False,
    )
```

profile of v0, /device:TPU:17, one launch (start us, length us, event | category | flops | bytes accessed | tf_op | source)
XLA Modules:
  0.0 149.3 jit_solution(8669574692586738322)
XLA Ops:
  0.6 142.1 %shard_map.41 = (bf16[2,3,2,1024,256]{4,3,2,1,0:T(8,128)(2,1)S(1)}, f32[4,128]{1,0:T(4,128)S(1)}) custom-call(bf16[2,3,8,64,1024]{4,3,2,1,0:T(8,128)(2,1)} %state.1, s32[8,64,1024]{2,1,0:T(8,128)} %shells.1), custom_call_target="tpu_custom_call" | custom-call | tf_op jit(solution)/shard_map/pallas_call | solution.py:235
  142.7 0.6 multiply_bitcast_fusion
  143.3 6.0 %convert_element_type.3 = f32[2,3,2,1024,256]{4,3,2,1,0:T(8,128)} convert(bf16[2,3,2,1024,256]{4,3,2,1,0:T(8,128)(2,1)S(1)} %get-tuple-element.4) | non-fusion elementwise | flops 3145728 | bytes 18874368 | tf_op jit(solution)/shard_map/convert_element_type | solution.py:270
where the time goes:
time: 152 us; the launch traced here: 149 us
  Pallas kernels  142 us (93%)
  other arithmetic  6.6 us (4%)
    pallas_call x1, Pallas kernels, local(): pl.pallas_call(functools.partial(kernel, slab_count, py_count, px_count),...  142 us
    convert_element_type x1, other arithmetic, local(): return (moved.astype(jnp.float32), spectrum)  6.02 us

commit v1 on v0

--- a/solution.py
+++ b/solution.py
@@ -13,10 +13,11 @@
 LANES = 128
 SPEC_ROWS = SHELLS // LANES
 GROUP_ROWS = 16
+CORES = 2
 MESH = pl.DeviceIdType.MESH
 
 
-def kernel(
+def move_kernel(
     slab_count,
     py_count,
     px_count,
@@ -24,28 +25,53 @@
     shells,
     out,
     spec,
+    moved,
     modes,
     labels,
     slab_parts,
     group_parts,
     state_sem,
     label_sem,
-    own_sem,
     send_sem,
     recv_sem,
     slab_send,
     slab_recv,
     part_send,
     part_recv,
+    ready_sem,
+    slab_ready,
 ):
     slab = lax.axis_index("slab")
     py = lax.axis_index("py")
     px = lax.axis_index("px")
     group = py_count * px_count
     me = py * px_count + px
+    cores = CORES if py_count % CORES == 0 else 1
     _, _, planes, rows, columns = state.shape
     planes_out = planes // py_count
     columns_out = columns // px_count
+
+    def position(any_py, any_px):
+        return (cores - 1 - any_py % cores, any_py // cores, any_px)
+
+    here = (cores - 1 - lax.rem(py, cores), py // cores, px)
+    everyone = [(q_py, q_px) for q_py in range(py_count) for q_px in range(px_count)]
+
+    def all_of(conditions):
+        return functools.reduce(jnp.logical_and, conditions)
+
+    def same(spot):
+        return all_of([a == b for a, b in zip(spot, here)])
+
+    def after_me(spot):
+        return jnp.logical_and(
+            all_of([a >= b for a, b in zip(spot, here)]), jnp.logical_not(same(spot))
+        )
+
+    def before_me(spot):
+        return jnp.logical_and(
+            all_of([a <= b for a, b in zip(spot, here)]), jnp.logical_not(same(spot))
+        )
 
     def load_state(z):
         return pltpu.make_async_copy(state.at[:, :, z], modes.at[:, :, z], state_sem.at[z])
@@ -69,13 +95,13 @@
             pl.ds(pl.multiple_of(dest_px * columns_out, columns_out), columns_out),
         ]
 
-    def landing(source):
-        return out.at[:, :, :, pl.ds(pl.multiple_of(source * rows, rows), rows), :]
+    def strip(buffer, source):
+        return buffer.at[:, :, :, pl.ds(pl.multiple_of(source * rows, rows), rows), :]
 
     def send_block(dest_py, dest_px):
         return pltpu.make_async_remote_copy(
             src_ref=block(state, dest_py, dest_px),
-            dst_ref=landing(me),
+            dst_ref=strip(moved, me),
             send_sem=send_sem.at[dest_py * px_count + dest_px],
             recv_sem=recv_sem.at[me],
             device_id=(slab, dest_py, dest_px),
@@ -85,28 +111,12 @@
     def take_block(source, source_py, source_px):
         return pltpu.make_async_remote_copy(
             src_ref=block(state, source_py, source_px),
-            dst_ref=landing(source),
+            dst_ref=strip(moved, source),
             send_sem=send_sem.at[source],
             recv_sem=recv_sem.at[source],
             device_id=(slab, source_py, source_px),
             device_id_type=MESH,
         )
-
-    def send_at(distance):
-        for turn in range(py_count):
-            dest_py = lax.rem(py + turn, py_count)
-            if distance == 0:
-                if turn > 0:
-                    send_block(dest_py, px).start()
-                continue
-
-            @pl.when(px + distance < px_count)
-            def _():
-                send_block(dest_py, px + distance).start()
-
-            @pl.when(px - distance >= 0)
-            def _():
-                send_block(dest_py, px - distance).start()
 
     def slab_copy(dest, slot):
         return pltpu.make_async_remote_copy(
@@ -128,24 +138,95 @@
             device_id_type=MESH,
         )
 
+    barrier = pltpu.get_barrier_semaphore()
+    for q_py, q_px in everyone:
+
+        @pl.when(after_me(position(q_py, q_px)))
+        def _():
+            pl.semaphore_signal(
+                barrier, inc=1, device_id=(slab, q_py, q_px), device_id_type=MESH
+            )
+
+    for q_slab in range(1, slab_count):
+
+        @pl.when(q_slab > slab)
+        def _():
+            pl.semaphore_signal(
+                barrier, inc=1, device_id=(q_slab, py, px), device_id_type=MESH
+            )
+
+    before = (here[0] + 1) * (here[1] + 1) * (here[2] + 1) - 1 + slab
+
+    @pl.when(before > 0)
+    def _():
+        pl.semaphore_wait(barrier, before)
+
+    def spot_of(dest_py, dest_px):
+        return (cores - 1 - lax.rem(dest_py, cores), dest_py // cores, dest_px)
+
+    def send_if(condition, dest_py, dest_px):
+        @pl.when(condition)
+        def _():
+            send_block(dest_py, dest_px).start()
+
+    def send_far(wanted):
+        for distance in range(px_count - 1, 1, -1):
+            for turn in range(py_count):
+                dest_py = lax.rem(py + turn, py_count)
+                for dest_px in (px + distance, px - distance):
+                    inside = jnp.logical_and(dest_px >= 0, dest_px < px_count)
+                    send_if(
+                        jnp.logical_and(inside, wanted(spot_of(dest_py, dest_px))),
+                        dest_py,
+                        dest_px,
+                    )
+
+    def send_near():
+        for turn in range(py_count):
+            dest_py = lax.rem(py + turn, py_count)
+            send_if(px - 1 >= 0, dest_py, px - 1)
+            if turn > 0:
+                send_if(px + 1 < px_count, dest_py, px + 1)
+        for turn in range(1, py_count):
+            send_block(lax.rem(py + turn, py_count), px).start()
+
+    def hear(wanted):
+        for q_py, q_px in everyone:
+            spot = position(q_py, q_px)
+
+            @pl.when(jnp.logical_and(after_me(spot), wanted(q_py, q_px)))
+            def _():
+                pl.semaphore_wait(ready_sem.at[q_py * px_count + q_px], 1)
+
+    send_far(before_me)
+
+    for q_py, q_px in everyone:
+
+        @pl.when(before_me(position(q_py, q_px)))
+        def _():
+            pl.semaphore_signal(
+                ready_sem.at[me], inc=1, device_id=(slab, q_py, q_px), device_id_type=MESH
+            )
+
+    for q_slab in range(slab_count - 1):
+
+        @pl.when(q_slab < slab)
+        def _():
+            pl.semaphore_signal(
+                slab_ready.at[slab], inc=1, device_id=(q_slab, py, px), device_id_type=MESH
+            )
+
+    def is_next(q_py, q_px):
+        return jnp.logical_and(q_py == py, q_px == px + 1)
+
+    hear(is_next)
+    send_if(px + 1 < px_count, py, px + 1)
+    hear(lambda q_py, q_px: jnp.logical_not(is_next(q_py, q_px)))
+    send_far(lambda spot: jnp.logical_not(before_me(spot)))
+
     for z in range(planes):
         load_state(z).start()
         load_labels(z).start()
-
-    barrier = pltpu.get_barrier_semaphore()
-    for step in range(1, group):
-        _, peer_py, peer_px = group_peer(step)
-        pl.semaphore_signal(
-            barrier, inc=1, device_id=(slab, peer_py, peer_px), device_id_type=MESH
-        )
-    for step in range(1, slab_count):
-        pl.semaphore_signal(
-            barrier, inc=1, device_id=(slab_peer(step), py, px), device_id_type=MESH
-        )
-    pl.semaphore_wait(barrier, group - 1 + slab_count - 1)
-
-    for distance in range(px_count - 1, 0, -1):
-        send_at(distance)
 
     low_ids = lax.broadcasted_iota(jnp.int32, (LOW, columns), 0)
     high_ids = lax.broadcasted_iota(jnp.int32, (HIGH, columns), 0)
@@ -175,9 +256,6 @@
         load_state(z).wait()
         load_labels(z).wait()
 
-    own = pltpu.make_async_copy(block(state, py, px), landing(me), own_sem)
-    own.start()
-
     groups = rows // GROUP_ROWS
     running = lax.fori_loop(
         0,
@@ -194,6 +272,12 @@
         slab_parts[slab, high // per_row : high // per_row + 1, lane : lane + LOW] = part[
             high : high + 1
         ]
+
+    for q_slab in range(1, slab_count):
+
+        @pl.when(q_slab > slab)
+        def _():
+            pl.semaphore_wait(slab_ready.at[q_slab], 1)
 
     for step in range(1, slab_count):
         slab_copy(slab_peer(step), slab).start()
@@ -206,7 +290,17 @@
     for step in range(1, group):
         part_copy(*group_peer(step), me).start()
 
-    send_at(0)
+    send_near()
+
+    def widen(source, target):
+        for real in range(source.shape[0]):
+            for part_of in range(source.shape[1]):
+                for plane in range(source.shape[2]):
+                    target[real, part_of, plane] = source[real, part_of, plane].astype(
+                        jnp.float32
+                    )
+
+    widen(block(modes, py, px), strip(out, me))
 
     for step in range(1, group):
         peer, peer_py, peer_px = group_peer(step)
@@ -214,16 +308,55 @@
     total = group_parts[0]
     for slot in range(1, group):
         total = total + group_parts[slot]
-    spec[...] = total
-
-    own.wait()
+    modes_all = planes * rows * columns * slab_count * group
+    spec[...] = total * (SHELLS / modes_all)
+
+    def take_and_widen(source_py, source_px):
+        source = source_py * px_count + source_px
+        take_block(source, source_py, source_px).wait_recv()
+        widen(strip(moved, source), strip(out, source))
+
     for step in range(1, slab_count):
         slab_copy(slab_peer(step), slab).wait_send()
     for step in range(1, group):
         peer, peer_py, peer_px = group_peer(step)
         part_copy(peer, peer_py, peer_px, me).wait_send()
+
+    half = px_count // 2
+    ahead = jnp.where(px < half, 1, px_count - 1)
+
+    def take_step(step, carry):
+        source_px = lax.rem(px + ahead * (half + step // py_count), px_count)
+        source_py = lax.rem(py + py_count - lax.rem(step, py_count), py_count)
+
+        @pl.when(jnp.logical_or(source_px != px, source_py != py))
+        def _():
+            take_and_widen(source_py, source_px)
+
+        return carry
+
+    lax.fori_loop(0, group, take_step, 0)
+    for step in range(1, group):
+        _, peer_py, peer_px = group_peer(step)
         send_block(peer_py, peer_px).wait_send()
-        take_block(peer, peer_py, peer_px).wait_recv()
+
+
+def store_kernel(widened, totals, out, spectrum, out_sem, spectrum_sem):
+    pieces = [
+        (real, part, plane)
+        for real in range(widened.shape[0])
+        for part in range(widened.shape[1])
+        for plane in range(widened.shape[2])
+    ]
+    copies = [
+        pltpu.make_async_copy(widened.at[piece], out.at[piece], out_sem.at[i])
+        for i, piece in enumerate(pieces)
+    ]
+    copies.append(pltpu.make_async_copy(totals, spectrum, spectrum_sem))
+    for copy in copies:
+        copy.start()
+    for copy in copies:
+        copy.wait()
 
 
 def local(state, shells):
@@ -232,13 +365,12 @@
     px_count = lax.axis_size("px")
     group = py_count * px_count
     _, _, planes, rows, columns = state.shape
-    moved, totals = pl.pallas_call(
-        functools.partial(kernel, slab_count, py_count, px_count),
+    moved_shape = (2, 3, planes // py_count, rows * group, columns // px_count)
+    widened, totals = pl.pallas_call(
+        functools.partial(move_kernel, slab_count, py_count, px_count),
         out_shape=(
-            pltpu.VMEM(
-                (2, 3, planes // py_count, rows * group, columns // px_count), state.dtype
-            ),
-            jax.ShapeDtypeStruct((SPEC_ROWS, LANES), jnp.float32),
+            pltpu.VMEM(moved_shape, jnp.float32),
+            pltpu.VMEM((SPEC_ROWS, LANES), jnp.float32),
         ),
         in_specs=[pl.BlockSpec(memory_space=pl.ANY)] * 2,
         out_specs=(
@@ -246,28 +378,49 @@
             pl.BlockSpec(memory_space=pltpu.VMEM),
         ),
         scratch_shapes=[
+            pltpu.VMEM(moved_shape, state.dtype),
             pltpu.VMEM(state.shape, state.dtype),
             pltpu.VMEM(shells.shape, shells.dtype),
             pltpu.VMEM((slab_count, SPEC_ROWS, LANES), jnp.float32),
             pltpu.VMEM((group, SPEC_ROWS, LANES), jnp.float32),
             pltpu.SemaphoreType.DMA((planes,)),
             pltpu.SemaphoreType.DMA((planes,)),
-            pltpu.SemaphoreType.DMA,
             pltpu.SemaphoreType.DMA((group,)),
             pltpu.SemaphoreType.DMA((group,)),
             pltpu.SemaphoreType.DMA((slab_count,)),
             pltpu.SemaphoreType.DMA((slab_count,)),
             pltpu.SemaphoreType.DMA((group,)),
             pltpu.SemaphoreType.DMA((group,)),
+            pltpu.SemaphoreType.REGULAR((group,)),
+            pltpu.SemaphoreType.REGULAR((slab_count,)),
         ],
-        compiler_params=pltpu.CompilerParams(collective_id=0, has_side_effects=True, vmem_limit_bytes=24 << 20),
+        name="move",
+        compiler_params=pltpu.CompilerParams(
+            collective_id=0, has_side_effects=True, vmem_limit_bytes=40 << 20
+        ),
     )(
         pltpu.with_memory_space_constraint(state, pltpu.HBM),
         pltpu.with_memory_space_constraint(shells, pltpu.HBM),
     )
-    modes_all = planes * rows * columns * slab_count * group
-    spectrum = totals.reshape(SHELLS) * (SHELLS / modes_all)
-    return (moved.astype(jnp.float32), spectrum)
+    restored, spectrum = pl.pallas_call(
+        store_kernel,
+        out_shape=(
+            jax.ShapeDtypeStruct(moved_shape, jnp.float32),
+            jax.ShapeDtypeStruct((SPEC_ROWS, LANES), jnp.float32),
+        ),
+        in_specs=[pl.BlockSpec(memory_space=pltpu.VMEM)] * 2,
+        out_specs=(
+            pl.BlockSpec(memory_space=pl.ANY),
+            pl.BlockSpec(memory_space=pl.ANY),
+        ),
+        scratch_shapes=[
+            pltpu.SemaphoreType.DMA((2 * 3 * (planes // py_count),)),
+            pltpu.SemaphoreType.DMA,
+        ],
+        name="store",
+        compiler_params=pltpu.CompilerParams(vmem_limit_bytes=40 << 20),
+    )(widened, totals)
+    return (restored, spectrum.reshape(SHELLS))
 
 
 def solution(mesh):

time: 152 us -> 146 us (0.961); the launches traced: 149 us -> 146 us
  other arithmetic: 6.6 us -> 0 us
  Pallas kernels: 142 us -> 146 us
    convert_element_type x1 -> x0, other arithmetic: 6.02 us -> none  [local(): return (moved.astype(jnp.float32), spectrum)]
    pallas_call x1 -> x2, Pallas kernels: 142 us -> 146 us  [the longest x1 141 us: local(): pl.pallas_call(functools.partial(move_kernel, slab_count, py_count, px_co...]
where the time goes in v1:
time: 146 us
  Pallas kernels  146 us (100%)
    pallas_call x1, Pallas kernels, local(): pl.pallas_call(functools.partial(move_kernel, slab_count, py_count, px_co...  141 us
    pallas_call x1, Pallas kernels, local(): pl.pallas_call(store_kernel, out_shape=(jax.ShapeDtypeStruct(moved_shape,...  4.68 us

profile of v1, /device:TPU:17, one launch (start us, length us, event | category | flops | bytes accessed | tf_op | source)
XLA Modules:
  0.0 146.2 jit_solution(10622892102889461440)
XLA Ops:
  0.6 140.9 %move.1 = (f32[2,3,2,1024,256]{4,3,2,1,0:T(8,128)S(1)}, f32[4,128]{1,0:T(4,128)S(1)}) custom-call(bf16[2,3,8,64,1024]{4,3,2,1,0:T(8,128)(2,1)} %state.1, s32[8,64,1024]{2,1,0:T(8,128)} %shells.1), custom_call_target="tpu_custom_call" | custom-call | tf_op jit(solution)/shard_map/move/pallas_call | solution.py:369
  141.5 4.7 %store.1 = (f32[2,3,2,1024,256]{4,3,2,1,0:T(8,128)}, f32[4,128]{1,0:T(4,128)}) custom-call(f32[2,3,2,1024,256]{4,3,2,1,0:T(8,128)S(1)} %get-tuple-element.6.widened, f32[4,128]{1,0:T(4,128)S(1)} %get-tuple-element.7.totals), custom_call_target="tpu_custom_call" | custom-call | tf_op jit(solution)/shard_map/store/pallas_call | solution.py:405

commit v2 on v1

--- a/solution.py
+++ b/solution.py
@@ -15,6 +15,76 @@
 GROUP_ROWS = 16
 CORES = 2
 MESH = pl.DeviceIdType.MESH
+
+
+def core_count(py_count):
+    return CORES if py_count % CORES == 0 else 1
+
+
+def inner_at(px, px_count):
+    half = px_count // 2
+    return jnp.logical_and(half > 0, jnp.logical_or(px == half - 1, px == half))
+
+
+def across(px, px_count):
+    return 2 * (px_count // 2) - 1 - px
+
+
+def is_late(py_count, px_count, py, px, dest_py, dest_px):
+    cores = core_count(py_count)
+    lasts = jnp.logical_and(lax.rem(py, cores) == cores - 1, lax.rem(dest_py, cores) == cores - 1)
+    mates = jnp.logical_and(inner_at(px, px_count), dest_px == across(px, px_count))
+    return jnp.logical_and(cores > 1, jnp.logical_and(lasts, mates))
+
+
+def swap_kernel(py_count, px_count, state, after, rest, moved, send_sem, recv_sem):
+    slab = lax.axis_index("slab")
+    py = lax.axis_index("py")
+    px = lax.axis_index("px")
+    cores = core_count(py_count)
+    chips = py_count // cores
+    _, _, planes, rows, columns = state.shape
+    planes_out = planes // py_count
+    columns_out = columns // px_count
+    mate = across(px, px_count)
+
+    def copy(chip, slot):
+        return pltpu.make_async_remote_copy(
+            src_ref=state.at[
+                :,
+                :,
+                pl.ds((chip * cores + cores - 1) * planes_out, planes_out),
+                :,
+                pl.ds(pl.multiple_of(mate * columns_out, columns_out), columns_out),
+            ],
+            dst_ref=moved.at[slot],
+            send_sem=send_sem.at[chip],
+            recv_sem=recv_sem.at[slot],
+            device_id=(slab, chip * cores + cores - 1, mate),
+            device_id_type=MESH,
+        )
+
+    @pl.when(is_late(py_count, px_count, py, px, cores - 1, mate))
+    def _():
+        here = py // cores
+        barrier = pltpu.get_barrier_semaphore()
+        for chip in range(chips):
+            pl.semaphore_signal(
+                barrier, inc=1, device_id=(slab, chip * cores + cores - 1, mate), device_id_type=MESH
+            )
+        pl.semaphore_wait(barrier, chips)
+        for turn in range(chips):
+            copy(lax.rem(here + turn, chips), here).start()
+        for turn in range(chips):
+            chip = lax.rem(here + chips - turn, chips)
+            copy(chip, chip).wait_recv()
+            for real in range(moved.shape[1]):
+                for part in range(moved.shape[2]):
+                    for plane in range(planes_out):
+                        piece = (chip, real, part, plane)
+                        rest[piece] = moved[piece].astype(jnp.float32)
+        for chip in range(chips):
+            copy(chip, here).wait_send()
 
 
 def move_kernel(
@@ -46,7 +116,7 @@
     px = lax.axis_index("px")
     group = py_count * px_count
     me = py * px_count + px
-    cores = CORES if py_count % CORES == 0 else 1
+    cores = core_count(py_count)
     _, _, planes, rows, columns = state.shape
     planes_out = planes // py_count
     columns_out = columns // px_count
@@ -164,41 +234,48 @@
     def spot_of(dest_py, dest_px):
         return (cores - 1 - lax.rem(dest_py, cores), dest_py // cores, dest_px)
 
+    def late(dest_py, dest_px):
+        return is_late(py_count, px_count, py, px, dest_py, dest_px)
+
     def send_if(condition, dest_py, dest_px):
-        @pl.when(condition)
+        @pl.when(jnp.logical_and(condition, jnp.logical_not(late(dest_py, dest_px))))
         def _():
             send_block(dest_py, dest_px).start()
+
+    def send_at(distance, wanted, turns=range(py_count)):
+        for turn in turns:
+            dest_py = lax.rem(py + turn, py_count)
+            for dest_px in (px + distance, px - distance):
+                inside = jnp.logical_and(dest_px >= 0, dest_px < px_count)
+                send_if(
+                    jnp.logical_and(inside, wanted(dest_py, dest_px)), dest_py, dest_px
+                )
 
     def send_far(wanted):
         for distance in range(px_count - 1, 1, -1):
-            for turn in range(py_count):
-                dest_py = lax.rem(py + turn, py_count)
-                for dest_px in (px + distance, px - distance):
-                    inside = jnp.logical_and(dest_px >= 0, dest_px < px_count)
-                    send_if(
-                        jnp.logical_and(inside, wanted(spot_of(dest_py, dest_px))),
-                        dest_py,
-                        dest_px,
-                    )
+            send_at(distance, wanted)
+
+    next_py = py + cores - 1 - 2 * lax.rem(py, cores)
+
+    def is_next(q_py, q_px):
+        return all_of([q_py == next_py, q_px == px + 1, q_px == px_count // 2])
 
     def send_near():
-        for turn in range(py_count):
-            dest_py = lax.rem(py + turn, py_count)
-            send_if(px - 1 >= 0, dest_py, px - 1)
-            if turn > 0:
-                send_if(px + 1 < px_count, dest_py, px + 1)
+        apart = [turn for turn in range(py_count) if turn % cores]
+        alike = [turn for turn in range(py_count) if turn % cores == 0]
+        send_at(1, lambda *dest: jnp.logical_not(is_next(*dest)), apart + alike)
         for turn in range(1, py_count):
             send_block(lax.rem(py + turn, py_count), px).start()
 
-    def hear(wanted):
-        for q_py, q_px in everyone:
-            spot = position(q_py, q_px)
-
-            @pl.when(jnp.logical_and(after_me(spot), wanted(q_py, q_px)))
+    def hear(rise_y, rise_px):
+        for core in range(cores):
+            spot = (core, here[1] + rise_y, px + rise_px)
+            q_py = spot[1] * cores + cores - 1 - core
+            exists = jnp.logical_and(q_py < py_count, spot[2] < px_count)
+
+            @pl.when(jnp.logical_and(exists, after_me(spot)))
             def _():
-                pl.semaphore_wait(ready_sem.at[q_py * px_count + q_px], 1)
-
-    send_far(before_me)
+                pl.semaphore_wait(ready_sem.at[q_py * px_count + spot[2]], 1)
 
     for q_py, q_px in everyone:
 
@@ -208,6 +285,8 @@
                 ready_sem.at[me], inc=1, device_id=(slab, q_py, q_px), device_id_type=MESH
             )
 
+    send_far(lambda *dest: before_me(spot_of(*dest)))
+
     for q_slab in range(slab_count - 1):
 
         @pl.when(q_slab < slab)
@@ -216,13 +295,22 @@
                 slab_ready.at[slab], inc=1, device_id=(q_slab, py, px), device_id_type=MESH
             )
 
-    def is_next(q_py, q_px):
-        return jnp.logical_and(q_py == py, q_px == px + 1)
-
-    hear(is_next)
-    send_if(px + 1 < px_count, py, px + 1)
-    hear(lambda q_py, q_px: jnp.logical_not(is_next(q_py, q_px)))
-    send_far(lambda spot: jnp.logical_not(before_me(spot)))
+    rises = [(y, x) for y in range(py_count // cores) for x in range(px_count)]
+    for rise_y, rise_px in sorted(rises, key=lambda rise: (sum(rise), rise[0])):
+        hear(rise_y, rise_px)
+
+        def reached(dest_py, dest_px):
+            return all_of(
+                [
+                    jnp.maximum(dest_py // cores - here[1], 0) == rise_y,
+                    jnp.maximum(dest_px - px, 0) == rise_px,
+                    jnp.logical_not(before_me(spot_of(dest_py, dest_px))),
+                ]
+            )
+
+        if rise_px == 1 and rise_y == 0:
+            send_if(is_next(next_py, px + 1), next_py, px + 1)
+        send_far(reached)
 
     for z in range(planes):
         load_state(z).start()
@@ -329,7 +417,10 @@
         source_px = lax.rem(px + ahead * (half + step // py_count), px_count)
         source_py = lax.rem(py + py_count - lax.rem(step, py_count), py_count)
 
-        @pl.when(jnp.logical_or(source_px != px, source_py != py))
+        other = jnp.logical_or(source_px != px, source_py != py)
+        here_now = jnp.logical_not(late(source_py, source_px))
+
+        @pl.when(jnp.logical_and(other, here_now))
         def _():
             take_and_widen(source_py, source_px)
 
@@ -338,25 +429,56 @@
     lax.fori_loop(0, group, take_step, 0)
     for step in range(1, group):
         _, peer_py, peer_px = group_peer(step)
-        send_block(peer_py, peer_px).wait_send()
-
-
-def store_kernel(widened, totals, out, spectrum, out_sem, spectrum_sem):
-    pieces = [
-        (real, part, plane)
-        for real in range(widened.shape[0])
-        for part in range(widened.shape[1])
-        for plane in range(widened.shape[2])
-    ]
-    copies = [
-        pltpu.make_async_copy(widened.at[piece], out.at[piece], out_sem.at[i])
-        for i, piece in enumerate(pieces)
-    ]
-    copies.append(pltpu.make_async_copy(totals, spectrum, spectrum_sem))
-    for copy in copies:
-        copy.start()
-    for copy in copies:
-        copy.wait()
+
+        @pl.when(jnp.logical_not(late(peer_py, peer_px)))
+        def _():
+            send_block(peer_py, peer_px).wait_send()
+
+
+def run_copies(copies, sems):
+    def each(act):
+        for i, (condition, source, target) in enumerate(copies):
+            copy = pltpu.make_async_copy(source, target, sems.at[i])
+            if condition is None:
+                act(copy)
+            else:
+                pl.when(condition)(functools.partial(act, copy))
+
+    each(lambda copy: copy.start())
+    each(lambda copy: copy.wait())
+
+
+def store_kernel(py_count, px_count, widened, totals, out, spectrum, sems):
+    py = lax.axis_index("py")
+    px = lax.axis_index("px")
+    rows = out.shape[3] // (py_count * px_count)
+    copies = [(None, totals, spectrum)]
+    for source_py in range(py_count):
+        for source_px in range(px_count):
+            start = (source_py * px_count + source_px) * rows
+            strip = (slice(None), slice(None), slice(None), pl.ds(start, rows))
+            missing = is_late(py_count, px_count, py, px, source_py, source_px)
+            copies.append((jnp.logical_not(missing), widened.at[strip], out.at[strip]))
+    run_copies(copies, sems)
+
+
+def rest_kernel(py_count, px_count, rest, stored, out, sems):
+    py = lax.axis_index("py")
+    px = lax.axis_index("px")
+    cores = core_count(py_count)
+    rows = rest.shape[4]
+    mate = across(px, px_count)
+    copies = []
+    for chip in range(py_count // cores):
+        start = pl.multiple_of(((chip * cores + cores - 1) * px_count + mate) * rows, rows)
+        copies.append(
+            (
+                is_late(py_count, px_count, py, px, chip * cores + cores - 1, mate),
+                rest.at[chip],
+                out.at[:, :, :, pl.ds(start, rows)],
+            )
+        )
+    run_copies(copies, sems)
 
 
 def local(state, shells):
@@ -402,24 +524,50 @@
         pltpu.with_memory_space_constraint(state, pltpu.HBM),
         pltpu.with_memory_space_constraint(shells, pltpu.HBM),
     )
-    restored, spectrum = pl.pallas_call(
-        store_kernel,
+    anywhere = pl.BlockSpec(memory_space=pl.ANY)
+    in_vmem = pl.BlockSpec(memory_space=pltpu.VMEM)
+    stored, spectrum = pl.pallas_call(
+        functools.partial(store_kernel, py_count, px_count),
         out_shape=(
             jax.ShapeDtypeStruct(moved_shape, jnp.float32),
             jax.ShapeDtypeStruct((SPEC_ROWS, LANES), jnp.float32),
         ),
-        in_specs=[pl.BlockSpec(memory_space=pltpu.VMEM)] * 2,
-        out_specs=(
-            pl.BlockSpec(memory_space=pl.ANY),
-            pl.BlockSpec(memory_space=pl.ANY),
-        ),
-        scratch_shapes=[
-            pltpu.SemaphoreType.DMA((2 * 3 * (planes // py_count),)),
-            pltpu.SemaphoreType.DMA,
-        ],
+        in_specs=[in_vmem] * 2,
+        out_specs=(anywhere, anywhere),
+        scratch_shapes=[pltpu.SemaphoreType.DMA((1 + group,))],
         name="store",
         compiler_params=pltpu.CompilerParams(vmem_limit_bytes=40 << 20),
     )(widened, totals)
+    chips = py_count // core_count(py_count)
+    rest_shape = (chips, 2, 3, planes // py_count, rows, columns // px_count)
+    rest = pl.pallas_call(
+        functools.partial(swap_kernel, py_count, px_count),
+        out_shape=pltpu.VMEM(rest_shape, jnp.float32),
+        in_specs=[anywhere] * 2,
+        out_specs=in_vmem,
+        scratch_shapes=[
+            pltpu.VMEM(rest_shape, state.dtype),
+            pltpu.SemaphoreType.DMA((chips,)),
+            pltpu.SemaphoreType.DMA((chips,)),
+        ],
+        name="swap",
+        compiler_params=pltpu.CompilerParams(
+            collective_id=1, has_side_effects=True, vmem_limit_bytes=40 << 20
+        ),
+    )(
+        pltpu.with_memory_space_constraint(state, pltpu.HBM),
+        pltpu.with_memory_space_constraint(spectrum, pltpu.HBM),
+    )
+    restored = pl.pallas_call(
+        functools.partial(rest_kernel, py_count, px_count),
+        out_shape=jax.ShapeDtypeStruct(moved_shape, jnp.float32),
+        in_specs=[in_vmem, anywhere],
+        out_specs=anywhere,
+        scratch_shapes=[pltpu.SemaphoreType.DMA((chips,))],
+        input_output_aliases={1: 0},
+        name="store_rest",
+        compiler_params=pltpu.CompilerParams(vmem_limit_bytes=40 << 20),
+    )(rest, stored)
     return (restored, spectrum.reshape(SHELLS))
 
 

time: 146 us -> 144 us (0.986)
  Pallas kernels: 146 us -> 143 us
    pallas_call x1, Pallas kernels: 141 us -> 125 us  [local(): pl.pallas_call(functools.partial(move_kernel, slab_count, py_count, px_co...]
    pallas_call x1 -> x3, Pallas kernels: 4.68 us -> 18.6 us  [the longest x1 13.2 us: local(): pl.pallas_call(functools.partial(swap_kernel, py_count, px_count), out_sh...]
where the time goes in v2:
time: 144 us
  Pallas kernels  143 us (99%)
    pallas_call x1, Pallas kernels, local(): pl.pallas_call(functools.partial(move_kernel, slab_count, py_count, px_co...  125 us
    pallas_call x1, Pallas kernels, local(): pl.pallas_call(functools.partial(swap_kernel, py_count, px_count), out_sh...  13.2 us
    pallas_call x1, Pallas kernels, local(): pl.pallas_call(functools.partial(store_kernel, py_count, px_count), out_s...  4.24 us

profile of v2, /device:TPU:17, one launch (start us, length us, event | category | flops | bytes accessed | tf_op | source)
XLA Modules:
  0.0 143.9 jit_solution(2447066597881682984)
XLA Ops:
  0.6 124.6 %move.1 = (f32[2,3,2,1024,256]{4,3,2,1,0:T(8,128)S(1)}, f32[4,128]{1,0:T(4,128)S(1)}) custom-call(bf16[2,3,8,64,1024]{4,3,2,1,0:T(8,128)(2,1)} %state.3, s32[8,64,1024]{2,1,0:T(8,128)} %shells.1), custom_call_target="tpu_custom_call" | custom-call | tf_op jit(solution)/shard_map/move/pallas_call | solution.py:491
  125.2 4.2 %store.1 = (f32[2,3,2,1024,256]{4,3,2,1,0:T(8,128)}, f32[4,128]{1,0:T(4,128)}) custom-call(f32[2,3,2,1024,256]{4,3,2,1,0:T(8,128)S(1)} %get-tuple-element.6.widened, f32[4,128]{1,0:T(4,128)S(1)} %get-tuple-element.7.totals), custom_call_target="tpu_custom_call" | custom-call | tf_op jit(solution)/shard_map/store/pallas_call | solution.py:529
  129.5 13.2 %swap.1.rest = f32[2,2,3,2,64,256]{5,4,3,2,1,0:T(8,128)S(1)} custom-call(bf16[2,3,8,64,1024]{4,3,2,1,0:T(8,128)(2,1)} %state.3, f32[4,128]{1,0:T(4,128)} %get-tuple-element.8.after), custom_call_target="tpu_custom_call" | custom-call | tf_op jit(solution)/shard_map/swap/pallas_call | solution.py:543
  142.7 1.2 store_rest.1

commit v3 on v2

--- a/solution.py
+++ b/solution.py
@@ -74,7 +74,7 @@
             )
         pl.semaphore_wait(barrier, chips)
         for turn in range(chips):
-            copy(lax.rem(here + turn, chips), here).start()
+            copy(turn, here).start()
         for turn in range(chips):
             chip = lax.rem(here + chips - turn, chips)
             copy(chip, chip).wait_recv()
@@ -125,7 +125,38 @@
         return (cores - 1 - any_py % cores, any_py // cores, any_px)
 
     here = (cores - 1 - lax.rem(py, cores), py // cores, px)
-    everyone = [(q_py, q_px) for q_py in range(py_count) for q_px in range(px_count)]
+    sizes = (cores, py_count // cores, px_count)
+    offsets = sorted(
+        (
+            (core, y, x)
+            for core in range(sizes[0])
+            for y in range(sizes[1])
+            for x in range(sizes[2])
+            if core + y + x > 0
+        ),
+        key=lambda offset: (offset[1] + offset[2], offset[1], offset[0]),
+    )
+
+    def tell_all(way, semaphore):
+        fits = [
+            [
+                (here[axis] + step < sizes[axis]) if way > 0 else (here[axis] >= step)
+                for step in range(sizes[axis])
+            ]
+            for axis in range(3)
+        ]
+        for offset in offsets:
+            core, y, x = (here[axis] + way * offset[axis] for axis in range(3))
+
+            @pl.when(all_of([fits[axis][offset[axis]] for axis in range(3) if offset[axis]]))
+            def _():
+                pl.semaphore_signal(
+                    semaphore,
+                    inc=1,
+                    device_id=(slab, y * cores + cores - 1 - core, x),
+                    device_id_type=MESH,
+                )
+
 
     def all_of(conditions):
         return functools.reduce(jnp.logical_and, conditions)
@@ -209,13 +240,7 @@
         )
 
     barrier = pltpu.get_barrier_semaphore()
-    for q_py, q_px in everyone:
-
-        @pl.when(after_me(position(q_py, q_px)))
-        def _():
-            pl.semaphore_signal(
-                barrier, inc=1, device_id=(slab, q_py, q_px), device_id_type=MESH
-            )
+    tell_all(1, barrier)
 
     for q_slab in range(1, slab_count):
 
@@ -260,12 +285,20 @@
     def is_next(q_py, q_px):
         return all_of([q_py == next_py, q_px == px + 1, q_px == px_count // 2])
 
+    def is_outward(q_py, q_px):
+        same_side = (q_px < px_count // 2) == (px < px_count // 2)
+        return jnp.logical_and(inner_at(px, px_count), same_side)
+
     def send_near():
         apart = [turn for turn in range(py_count) if turn % cores]
         alike = [turn for turn in range(py_count) if turn % cores == 0]
-        send_at(1, lambda *dest: jnp.logical_not(is_next(*dest)), apart + alike)
-        for turn in range(1, py_count):
-            send_block(lax.rem(py + turn, py_count), px).start()
+        send_at(
+            1,
+            lambda *dest: jnp.logical_not(
+                jnp.logical_or(is_next(*dest), is_outward(*dest))
+            ),
+            apart + alike,
+        )
 
     def hear(rise_y, rise_px):
         for core in range(cores):
@@ -277,13 +310,7 @@
             def _():
                 pl.semaphore_wait(ready_sem.at[q_py * px_count + spot[2]], 1)
 
-    for q_py, q_px in everyone:
-
-        @pl.when(before_me(position(q_py, q_px)))
-        def _():
-            pl.semaphore_signal(
-                ready_sem.at[me], inc=1, device_id=(slab, q_py, q_px), device_id_type=MESH
-            )
+    tell_all(-1, ready_sem.at[me])
 
     send_far(lambda *dest: before_me(spot_of(*dest)))
 
@@ -311,6 +338,10 @@
         if rise_px == 1 and rise_y == 0:
             send_if(is_next(next_py, px + 1), next_py, px + 1)
         send_far(reached)
+
+    send_at(1, is_outward)
+    for turn in range(1, py_count):
+        send_block(lax.rem(py + turn, py_count), px).start()
 
     for z in range(planes):
         load_state(z).start()

time: 144 us -> 142 us (0.986); the launches traced: 144 us -> 140 us
  Pallas kernels: 143 us -> 139 us
    pallas_call x1, Pallas kernels: 13.2 us -> 9.35 us  [local(): pl.pallas_call(functools.partial(swap_kernel, py_count, px_count), out_sh...]
where the time goes in v3:
time: 142 us; the launch traced here: 140 us
  Pallas kernels  139 us (98%)
    pallas_call x1, Pallas kernels, local(): pl.pallas_call(functools.partial(move_kernel, slab_count, py_count, px_co...  124 us
    pallas_call x1, Pallas kernels, local(): pl.pallas_call(functools.partial(swap_kernel, py_count, px_count), out_sh...  9.35 us
    pallas_call x1, Pallas kernels, local(): pl.pallas_call(functools.partial(store_kernel, py_count, px_count), out_s...  4.24 us

profile of v3, /device:TPU:17, one launch (start us, length us, event | category | flops | bytes accessed | tf_op | source)
XLA Modules:
  0.0 139.9 jit_solution(6504053085192207265)
XLA Ops:
  0.6 124.5 %move.1 = (f32[2,3,2,1024,256]{4,3,2,1,0:T(8,128)S(1)}, f32[4,128]{1,0:T(4,128)S(1)}) custom-call(bf16[2,3,8,64,1024]{4,3,2,1,0:T(8,128)(2,1)} %state.3, s32[8,64,1024]{2,1,0:T(8,128)} %shells.1), custom_call_target="tpu_custom_call" | custom-call | tf_op jit(solution)/shard_map/move/pallas_call | solution.py:522
  125.1 4.2 %store.1 = (f32[2,3,2,1024,256]{4,3,2,1,0:T(8,128)}, f32[4,128]{1,0:T(4,128)}) custom-call(f32[2,3,2,1024,256]{4,3,2,1,0:T(8,128)S(1)} %get-tuple-element.6.widened, f32[4,128]{1,0:T(4,128)S(1)} %get-tuple-element.7.totals), custom_call_target="tpu_custom_call" | custom-call | tf_op jit(solution)/shard_map/store/pallas_call | solution.py:560
  129.4 9.3 %swap.1.rest = f32[2,2,3,2,64,256]{5,4,3,2,1,0:T(8,128)S(1)} custom-call(bf16[2,3,8,64,1024]{4,3,2,1,0:T(8,128)(2,1)} %state.3, f32[4,128]{1,0:T(4,128)} %get-tuple-element.8.after), custom_call_target="tpu_custom_call" | custom-call | tf_op jit(solution)/shard_map/swap/pallas_call | solution.py:574
  138.7 1.2 store_rest.1

commit v4 on v3

--- a/solution.py
+++ b/solution.py
@@ -199,9 +199,9 @@
     def strip(buffer, source):
         return buffer.at[:, :, :, pl.ds(pl.multiple_of(source * rows, rows), rows), :]
 
-    def send_block(dest_py, dest_px):
+    def send_block(dest_py, dest_px, source=state):
         return pltpu.make_async_remote_copy(
-            src_ref=block(state, dest_py, dest_px),
+            src_ref=block(source, dest_py, dest_px),
             dst_ref=strip(moved, me),
             send_sem=send_sem.at[dest_py * px_count + dest_px],
             recv_sem=recv_sem.at[me],
@@ -262,18 +262,21 @@
     def late(dest_py, dest_px):
         return is_late(py_count, px_count, py, px, dest_py, dest_px)
 
-    def send_if(condition, dest_py, dest_px):
+    def send_if(condition, dest_py, dest_px, source=state):
         @pl.when(jnp.logical_and(condition, jnp.logical_not(late(dest_py, dest_px))))
         def _():
-            send_block(dest_py, dest_px).start()
-
-    def send_at(distance, wanted, turns=range(py_count)):
+            send_block(dest_py, dest_px, source).start()
+
+    def send_at(distance, wanted, turns=range(py_count), source=state):
         for turn in turns:
             dest_py = lax.rem(py + turn, py_count)
             for dest_px in (px + distance, px - distance):
                 inside = jnp.logical_and(dest_px >= 0, dest_px < px_count)
                 send_if(
-                    jnp.logical_and(inside, wanted(dest_py, dest_px)), dest_py, dest_px
+                    jnp.logical_and(inside, wanted(dest_py, dest_px)),
+                    dest_py,
+                    dest_px,
+                    source,
                 )
 
     def send_far(wanted):
@@ -298,6 +301,7 @@
                 jnp.logical_or(is_next(*dest), is_outward(*dest))
             ),
             apart + alike,
+            modes,
         )
 
     def hear(rise_y, rise_px):

time: 142 us -> 142 us (level)
  no operation moved by 1% of the time
where the time goes in v4:
time: 142 us; the launch traced here: 140 us
  Pallas kernels  139 us (98%)
    pallas_call x1, Pallas kernels, local(): pl.pallas_call(functools.partial(move_kernel, slab_count, py_count, px_co...  124 us
    pallas_call x1, Pallas kernels, local(): pl.pallas_call(functools.partial(swap_kernel, py_count, px_count), out_sh...  9.35 us
    pallas_call x1, Pallas kernels, local(): pl.pallas_call(functools.partial(store_kernel, py_count, px_count), out_s...  4.24 us

profile of v4, /device:TPU:17, one launch (start us, length us, event | category | flops | bytes accessed | tf_op | source)
XLA Modules:
  0.0 139.9 jit_solution(10740355250920196242)
XLA Ops:
  0.6 124.5 %move.1 = (f32[2,3,2,1024,256]{4,3,2,1,0:T(8,128)S(1)}, f32[4,128]{1,0:T(4,128)S(1)}) custom-call(bf16[2,3,8,64,1024]{4,3,2,1,0:T(8,128)(2,1)} %state.3, s32[8,64,1024]{2,1,0:T(8,128)} %shells.1), custom_call_target="tpu_custom_call" | custom-call | tf_op jit(solution)/shard_map/move/pallas_call | solution.py:526
  125.1 4.2 %store.1 = (f32[2,3,2,1024,256]{4,3,2,1,0:T(8,128)}, f32[4,128]{1,0:T(4,128)}) custom-call(f32[2,3,2,1024,256]{4,3,2,1,0:T(8,128)S(1)} %get-tuple-element.6.widened, f32[4,128]{1,0:T(4,128)S(1)} %get-tuple-element.7.totals), custom_call_target="tpu_custom_call" | custom-call | tf_op jit(solution)/shard_map/store/pallas_call | solution.py:564
  129.4 9.3 %swap.1.rest = f32[2,2,3,2,64,256]{5,4,3,2,1,0:T(8,128)S(1)} custom-call(bf16[2,3,8,64,1024]{4,3,2,1,0:T(8,128)(2,1)} %state.3, f32[4,128]{1,0:T(4,128)} %get-tuple-element.8.after), custom_call_target="tpu_custom_call" | custom-call | tf_op jit(solution)/shard_map/swap/pallas_call | solution.py:578
  138.7 1.2 store_rest.1
